TPU v7x, 256 devices: a whole 4x4x8 slice. The times are simulated.
256 devices in a mesh: dp: 8 (over x, core), expert: 32 (over z, y).
Axes of the slice: x: 4, y: 4, z: 8, core: 2. Of those that a mesh axis runs over, the one named last changes fastest.
Arguments:
- tokens: bfloat16 [32768, 1024], P(('dp', 'expert')), may hold values from -6 to 6
- route_a: int32 [32768, 1], P(('dp', 'expert')), may hold values from 0 to 31
- route_b: int32 [32768, 1], P(('dp', 'expert')), may hold values from 0 to 63
- gain_a: float32 [1024], replicated, may hold values from 0.25 to 1.75
- gain_b: float32 [1024], replicated, may hold values from 0.25 to 1.75
- router_a: bfloat16 [1024, 32], replicated, may hold values from -0.375 to 0.375
- router_b: bfloat16 [1024, 64], replicated, may hold values from -0.375 to 0.375
- dense_in_a: bfloat16 [1024, 4096], P(None, 'dp'), may hold values from -0.1875 to 0.1875
- dense_out_a: bfloat16 [4096, 1024], P('dp'), may hold values from -0.09375 to 0.09375
- dense_in_b: bfloat16 [1024, 4096], P(None, 'dp'), may hold values from -0.1875 to 0.1875
- dense_out_b: bfloat16 [4096, 1024], P('dp'), may hold values from -0.09375 to 0.09375
- expert_in_a: bfloat16 [32, 1024, 4096], P('expert', None, 'dp'), may hold values from -0.1875 to 0.1875
- expert_out_a: bfloat16 [32, 4096, 1024], P('expert', 'dp'), may hold values from -0.09375 to 0.09375
- expert_in_b: bfloat16 [64, 1024, 4096], P('expert', None, 'dp'), may hold values from -0.1875 to 0.1875
- expert_out_b: bfloat16 [64, 4096, 1024], P('expert', 'dp'), may hold values from -0.09375 to 0.09375
Outputs:
- stream_out: bfloat16 [32768, 1024], P(('dp', 'expert'))
All inputs are finite; a program needn't handle non-finite values.
Results may differ from a plain program's by a relative error of at most 0.0091.
Values may be sent and summed in bfloat16 or wider, within the bound.
A program may use at most 128 MiB of HBM per device.

v0:
```python
import jax
import jax.numpy as jnp
from jax import lax
from jax.sharding import PartitionSpec as P


def in_order(blocks, dim):
    shape = list(blocks.shape[1:])
    shape[dim] *= blocks.shape[0]
    return jnp.moveaxis(blocks, 0, dim).reshape(shape)


def from_everyone(value, axis):
    copies = jnp.broadcast_to(value, (lax.axis_size(axis), *value.shape))
    return lax.all_to_all(copies, axis, split_axis=0, concat_axis=0, tiled=True)


def gather_directly(value, axis, dim):
    return in_order(from_everyone(value, axis), dim)


def in_blocks(value, dim, devices):
    before, after = (value.shape[:dim], value.shape[dim + 1 :])
    return jnp.moveaxis(value.reshape(*before, devices, -1, *after), dim, 0)


def summed_on_arrival(value, axis, dim):
    devices = lax.axis_size(axis)
    blocks = lax.all_to_all(in_blocks(value, dim, devices), axis, 0, 0, tiled=True)
    return jnp.sum(blocks.astype(jnp.float32), axis=0)


def norm_rows(x, gain):
    xf = x.astype(jnp.float32)
    mean = jnp.mean(xf, axis=-1, keepdims=True)
    var = jnp.mean((xf - mean) ** 2, axis=-1, keepdims=True)
    return ((xf - mean) / jnp.sqrt(var + 1e-05) * gain).astype(jnp.bfloat16)


def rank_table(blocks, experts):
    onehot = (blocks[:, :, None] == jnp.arange(experts)[None, None, :]).astype(jnp.int32)
    before = jnp.cumsum(onehot, axis=1) - onehot
    rank = jnp.sum(before * onehot, axis=-1)
    return (onehot, rank)


def moe_layer(x, ids, gain, router, d_in, d_out, e_in, e_out):
    tok_rows, width = x.shape
    experts = router.shape[1]
    owners = lax.axis_size("expert")
    per_dev = experts // owners
    cap = (5 * tok_rows + 4 * experts - 1) // (4 * experts)
    normed = norm_rows(x, gain)
    onehot, rank = rank_table(ids.reshape(1, tok_rows), experts)
    rank = rank.reshape(-1)
    kept = rank < cap
    total = experts * cap
    slot_row = jnp.where(kept, ids * cap + rank, total)
    logits = jnp.dot(normed, router, preferred_element_type=jnp.float32)
    picked = jnp.sum(logits * onehot.reshape(-1, experts).astype(jnp.float32), axis=-1)
    gate = jax.nn.sigmoid(picked) * kept.astype(jnp.float32)
    dense_act = jax.nn.gelu(
        jnp.dot(gather_directly(normed, "dp", 0), d_in, preferred_element_type=jnp.float32),
        approximate=True,
    ).astype(jnp.bfloat16)
    rows = dense_act
    dense = summed_on_arrival(
        jnp.dot(rows, d_out, preferred_element_type=jnp.float32).astype(jnp.bfloat16), "dp", 0
    )
    buffer = jnp.zeros((total, width), jnp.bfloat16).at[slot_row].set(normed, mode="drop")
    buffer = buffer.reshape(owners, per_dev, cap, width)
    arrived = lax.all_to_all(buffer, "expert", split_axis=0, concat_axis=0, tiled=True)
    expert_act = jax.nn.gelu(
        jnp.einsum(
            "secd,edf->secf",
            lax.all_gather(arrived, "dp", axis=0, tiled=True),
            e_in,
            preferred_element_type=jnp.float32,
        ),
        approximate=True,
    ).astype(jnp.bfloat16)
    rows = expert_act
    partial_value = lax.psum_scatter(
        jnp.einsum("secf,efd->secd", rows, e_out, preferred_element_type=jnp.float32).astype(
            jnp.bfloat16
        ),
        "dp",
        scatter_dimension=0,
        tiled=True,
    ).astype(jnp.float32)
    returned = (
        lax.all_to_all(
            partial_value.astype(jnp.bfloat16), "expert", split_axis=0, concat_axis=0, tiled=True
        )
        .astype(partial_value.dtype)
        .reshape(total, width)
    )
    expert_tok = jnp.take(returned, slot_row, axis=0, mode="fill", fill_value=0.0)
    return (x.astype(jnp.float32) + dense + gate[:, None] * expert_tok).astype(jnp.bfloat16)


def body(
    tokens,
    route_a,
    route_b,
    gain_a,
    gain_b,
    router_a,
    router_b,
    dense_in_a,
    dense_out_a,
    dense_in_b,
    dense_out_b,
    expert_in_a,
    expert_out_a,
    expert_in_b,
    expert_out_b,
):
    middle = moe_layer(
        tokens, route_a[:, 0], gain_a, router_a, dense_in_a, dense_out_a, expert_in_a, expert_out_a
    )
    return moe_layer(
        middle, route_b[:, 0], gain_b, router_b, dense_in_b, dense_out_b, expert_in_b, expert_out_b
    )


def solution(mesh):
    in_specs = (
        P(("dp", "expert"), None),
        P(("dp", "expert"), None),
        P(("dp", "expert"), None),
        P(),
        P(),
        P(),
        P(),
        P(None, "dp"),
        P("dp", None),
        P(None, "dp"),
        P("dp", None),
        P("expert", None, "dp"),
        P("expert", "dp", None),
        P("expert", None, "dp"),
        P("expert", "dp", None),
    )
    out_specs = P(("dp", "expert"), None)
    return jax.shard_map(body, mesh=mesh, in_specs=in_specs, out_specs=out_specs, check_vma=False)
```

profile of v0, /device:TPU:32, one launch (start us, length us, event | category | flops | bytes accessed | tf_op | source)
XLA Modules:
  0.0 354.0 jit_solution(15019719602853124694)
XLA Ops:
  6.5 0.9 fusion.83
  7.4 0.2 reduce_window_sum.22
  7.6 0.8 select_reduce_fusion.1
  8.4 0.7 and_bitcast_fusion.1
  9.1 1.1 convert_reduce_fusion.3
  10.2 1.2 fusion.71
  11.4 1.8 scatter_custom_fusion
  13.1 0.1 reshape.321
  13.3 28.4 %all_to_all.40 = bf16[32,1,5,1024]{3,2,1,0:T(8,128)(2,1)S(1)} all-to-all(bf16[32,1,5,1024]{3,2,1,0:T(8,128)(2,1)S(1)} %bitcast.99), channel_id=1, replica_groups=mesh['dp'=8,'expert'=32] {'expert'}, dimensions={0} | all-to-all | bytes 655360 | tf_op jit(solution)/shard_map/all_to_all | solution.py:72
  41.6 0.9 copy.33
  42.6 0.0 all-gather.3.cloned.1.call-update
  42.6 0.0 reduce-scatter.3.cloned.1.call-start
  42.6 25.1 %all-gather.3.cloned.1.call-done = bf16[256,1,5,1024]{3,0,2,1:T(8,128)(2,1)} async-done(((bf16[32,1,5,1024]{3,0,2,1:T(8,128)(2,1)}), bf16[256,1,5,1024]{3,0,2,1:T(8,128)(2,1)}) %all-gather.3.cloned.1.call-update) | async-done | bytes 2621456 | tf_op jit(solution)/shard_map/all_gather | solution.py:76
  67.7 7.1 %convert_bitcast_fusion.1 = bf16[256,1,5,1024]{3,0,2,1:T(8,128)(2,1)} fusion(bf16[1,512,1024]{2,1,0:T(8,128)(2,1)} %param.27, bf16[256,1,5,1024]{3,0,2,1:T(8,128)(2,1)} %all-gather.3.cloned.1.call-done, bf16[1,1024,512]{2,1,0:T(8,128)(2,1)} %param.26), kind=kOutput, calls=%fused_computation.29 | convolution fusion | flops 2691563520 | bytes 7340032 | tf_op jit(solution)/shard_map/secf,efd->secd/dot_general | solution.py:84
  74.9 0.0 reduce-scatter.3.cloned.1.call-update
  74.9 0.9 copy-done.1
  75.8 0.2 fusion.73
  76.0 0.3 broadcast_in_dim.49
  76.2 39.3 %all_to_all.41 = bf16[8,128,1024]{2,1,0:T(8,128)(2,1)} all-to-all(bf16[8,128,1024]{2,1,0:T(8,128)(2,1)S(1)} %broadcast_in_dim.49), channel_id=1, replica_groups=mesh['dp'=8,'expert'=32] {'dp'}, dimensions={0} | all-to-all | bytes 4194304 | tf_op jit(solution)/shard_map/all_to_all | solution.py:15
  115.5 6.2 %convolution_convert_fusion.1 = bf16[1024,1024]{1,0:T(8,128)(2,1)} fusion(bf16[512,1024]{1,0:T(8,128)(2,1)} %param.23, bf16[1024,1024]{1,0:T(8,128)(2,1)} %bitcast.97, bf16[1024,512]{1,0:T(8,128)(2,1)} %param.22), kind=kOutput, calls=%fused_computation.50 | convolution fusion | flops 2153250816 | bytes 6291456 | tf_op jit(solution)/shard_map/dot_general | solution.py:68
  121.7 4.5 %all-to-all-start.1 = ((bf16[8,128,1024]{2,1,0:T(8,128)(2,1)}), bf16[8,128,1024]{2,1,0:T(8,128)(2,1)}, u32[]{:S(2)}, u32[]{:S(2)}) async-start(bf16[8,128,1024]{2,1,0:T(8,128)(2,1)} %bitcast.95), calls=%async_computation.1 | async-start | bytes 4194304 | tf_op jit(solution)/shard_map/all_to_all | solution.py:29
  126.2 0.1 fusion.82
  126.3 0.2 reduce_window_sum.23
  126.5 0.2 select_reduce_fusion
  126.7 0.2 fusion.45
  126.9 0.0 reduce-scatter.3.cloned.1.call-done
  126.9 2.0 copy.34
  128.9 24.5 %all-to-all-done.1 = bf16[8,128,1024]{2,1,0:T(8,128)(2,1)} async-done(((bf16[8,128,1024]{2,1,0:T(8,128)(2,1)}), bf16[8,128,1024]{2,1,0:T(8,128)(2,1)}, u32[]{:S(2)}, u32[]{:S(2)}) %all-to-all-start.1) | async-done | bytes 2097184 | tf_op jit(solution)/shard_map/all_to_all | solution.py:29
  153.4 10.1 %all-to-all-start.3 = ((bf16[32,1,5,1024]{3,2,1,0:T(8,128)(2,1)}), bf16[32,1,5,1024]{3,2,1,0:T(8,128)(2,1)}, u32[]{:S(2)}, u32[]{:S(2)}) async-start(bf16[32,1,5,1024]{3,2,1,0:T(8,128)(2,1)} %copy.34), calls=%async_computation.4 | async-start | bytes 1048576 | tf_op jit(solution)/shard_map/all_to_all | solution.py:92
  163.5 0.0 all-gather.5.cloned.1.call-start
  163.6 2.8 convert_reduce_fusion.1
  166.4 14.1 %all-to-all-done.3 = bf16[32,1,5,1024]{3,2,1,0:T(8,128)(2,1)} async-done(((bf16[32,1,5,1024]{3,2,1,0:T(8,128)(2,1)}), bf16[32,1,5,1024]{3,2,1,0:T(8,128)(2,1)}, u32[]{:S(2)}, u32[]{:S(2)}) %all-to-all-start.3) | async-done | bytes 327712 | tf_op jit(solution)/shard_map/all_to_all | solution.py:92
  180.5 1.2 reshape.334
  181.6 0.0 copy-start.5
  181.7 1.6 gather_fusion
  183.2 1.4 convert_reduce_fusion.2
  184.7 0.2 fusion.68
  184.9 1.4 scatter_custom_fusion.1
  186.3 0.2 reshape.330
  186.5 0.3 copy.35
  186.9 18.9 %all_to_all.42 = bf16[32,2,3,1024]{3,1,2,0:T(2,128)(2,1)S(1)} all-to-all(bf16[32,2,3,1024]{3,1,2,0:T(2,128)(2,1)S(1)} %copy.35), channel_id=1, replica_groups=mesh['dp'=8,'expert'=32] {'expert'}, dimensions={0} | all-to-all | bytes 786432 | tf_op jit(solution)/shard_map/all_to_all | solution.py:72
  205.7 0.8 copy.36
  206.6 0.0 all-gather.5.cloned.1.call-update
  206.6 0.2 reduce-scatter.5.cloned.1.call-start
  206.8 24.4 %all-gather.5.cloned.1.call-done = bf16[256,2,3,1024]{3,0,2,1:T(8,128)(2,1)} async-done(((bf16[32,2,3,1024]{3,0,2,1:T(8,128)(2,1)}), bf16[256,2,3,1024]{3,0,2,1:T(8,128)(2,1)}) %all-gather.5.cloned.1.call-update) | async-done | bytes 3145744 | tf_op jit(solution)/shard_map/all_gather | solution.py:76
  231.2 7.9 %convert_bitcast_fusion = bf16[256,2,3,1024]{3,0,2,1:T(8,128)(2,1)} fusion(bf16[2,512,1024]{2,1,0:T(8,128)(2,1)S(1)} %copy-done, bf16[256,2,3,1024]{3,0,2,1:T(8,128)(2,1)} %all-gather.5.cloned.1.call-done, bf16[2,1024,512]{2,1,0:T(8,128)(2,1)} %param.28), kind=kOutput, calls=%fused_computation.16 | convolution fusion | flops 3229876224 | bytes 10485760 | tf_op jit(solution)/shard_map/secf,efd->secd/dot_general | solution.py:84
  239.1 0.0 reduce-scatter.5.cloned.1.call-update
  239.1 0.2 fusion.70
  239.3 0.3 broadcast_in_dim.54
  239.5 38.7 %all_to_all.43 = bf16[8,128,1024]{2,1,0:T(8,128)(2,1)} all-to-all(bf16[8,128,1024]{2,1,0:T(8,128)(2,1)S(1)} %broadcast_in_dim.54), channel_id=1, replica_groups=mesh['dp'=8,'expert'=32] {'dp'}, dimensions={0} | all-to-all | bytes 4194304 | tf_op jit(solution)/shard_map/all_to_all | solution.py:15
  278.3 6.2 %convolution_convert_fusion = bf16[1024,1024]{1,0:T(8,128)(2,1)} fusion(bf16[512,1024]{1,0:T(8,128)(2,1)} %param.25, bf16[1024,1024]{1,0:T(8,128)(2,1)} %bitcast.98, bf16[1024,512]{1,0:T(8,128)(2,1)} %param.24), kind=kOutput, calls=%fused_computation.49 | convolution fusion | flops 2153250816 | bytes 6291456 | tf_op jit(solution)/shard_map/dot_general | solution.py:68
  284.5 4.5 %all-to-all-start.5 = ((bf16[8,128,1024]{2,1,0:T(8,128)(2,1)}), bf16[8,128,1024]{2,1,0:T(8,128)(2,1)}, u32[]{:S(2)}, u32[]{:S(2)}) async-start(bf16[8,128,1024]{2,1,0:T(8,128)(2,1)} %bitcast.96), calls=%async_computation.6 | async-start | bytes 4194304 | tf_op jit(solution)/shard_map/all_to_all | solution.py:29
  289.0 0.9 reduce-scatter.5.cloned.1.call-done
  289.9 2.1 copy.37
  292.0 24.2 %all-to-all-done.5 = bf16[8,128,1024]{2,1,0:T(8,128)(2,1)} async-done(((bf16[8,128,1024]{2,1,0:T(8,128)(2,1)}), bf16[8,128,1024]{2,1,0:T(8,128)(2,1)}, u32[]{:S(2)}, u32[]{:S(2)}) %all-to-all-start.5) | async-done | bytes 2097184 | tf_op jit(solution)/shard_map/all_to_all | solution.py:29
  316.1 10.1 %all-to-all-start.7 = ((bf16[32,2,3,1024]{3,1,2,0:T(2,128)(2,1)}), bf16[32,2,3,1024]{3,1,2,0:T(2,128)(2,1)S(1)}, u32[]{:S(2)}, u32[]{:S(2)}) async-start(bf16[32,2,3,1024]{3,1,2,0:T(2,128)(2,1)} %copy.37), calls=%async_computation.9 | async-start | bytes 786432 | tf_op jit(solution)/shard_map/all_to_all | solution.py:92
  326.3 0.2 fusion.44
  326.5 2.8 convert_reduce_fusion
  329.3 11.3 %all-to-all-done.7 = bf16[32,2,3,1024]{3,1,2,0:T(2,128)(2,1)S(1)} async-done(((bf16[32,2,3,1024]{3,1,2,0:T(2,128)(2,1)}), bf16[32,2,3,1024]{3,1,2,0:T(2,128)(2,1)S(1)}, u32[]{:S(2)}, u32[]{:S(2)}) %all-to-all-start.7) | async-done | bytes 393248 | tf_op jit(solution)/shard_map/all_to_all | solution.py:92
  340.6 0.1 copy_convert_fusion
  340.7 1.5 copy.39
  342.3 1.6 reshape.336
  343.9 1.6 gather_fusion.1
  345.4 2.0 fusion.77
  (24 shorter events, 0.1 us)
Async XLA Ops:
  6.5 224.7 %copy-start = (bf16[2,512,1024]{2,1,0:T(8,128)(2,1)S(1)}, bf16[2,512,1024]{2,1,0:T(8,128)(2,1)}, u32[]{:S(2)}) copy-start(bf16[2,512,1024]{2,1,0:T(8,128)(2,1)} %param.29) | copy-start | bytes 6291460
  6.5 61.2 %all-gather.3.cloned.1.call-start = ((), (), s32[]{:S(2)}) async-start(), calls=%async_computation.10 | async-start | bytes 2949120 | tf_op jit(solution)/shard_map/all_gather | solution.py:76
  42.6 84.3 %reduce-scatter.3.cloned.1.call-start = ((), (), s32[]{:S(2)}) async-start(), calls=%async_computation.11 | async-start | bytes 2949120 | tf_op jit(solution)/shard_map/reduce_scatter | solution.py:83
  74.9 0.9 copy-start.1
  74.9 1.0 copy-start.4
  121.7 4.5 %copy-start.7 = (s32[128,1]{0,1:T(1,128)S(1)}, s32[128,1]{0,1:T(1,128)}, u32[]{:S(2)}) copy-start(s32[128,1]{0,1:T(1,128)} %param.17) | copy-start | bytes 1540
  121.7 5.0 %copy-start.3 = (bf16[1024,32]{0,1:T(8,128)(2,1)S(1)}, bf16[1024,32]{0,1:T(8,128)(2,1)}, u32[]{:S(2)}) copy-start(bf16[1024,32]{0,1:T(8,128)(2,1)} %param.20) | copy-start | bytes 196612
  121.7 5.0 %copy-start.6 = (s32[128,1]{0,1:T(1,128)S(1)}, s32[128,1]{0,1:T(1,128)}, u32[]{:S(2)}) copy-start(s32[128,1]{0,1:T(1,128)} %param.16) | copy-start | bytes 1540
  121.7 31.7 %all-to-all-start.1 = ((bf16[8,128,1024]{2,1,0:T(8,128)(2,1)}), bf16[8,128,1024]{2,1,0:T(8,128)(2,1)}, u32[]{:S(2)}, u32[]{:S(2)}) async-start(bf16[8,128,1024]{2,1,0:T(8,128)(2,1)} %bitcast.95), calls=%async_computation.1 | async-start | bytes 4194304 | tf_op jit(solution)/shard_map/all_to_all | solution.py:29
  153.4 27.1 %all-to-all-start.3 = ((bf16[32,1,5,1024]{3,2,1,0:T(8,128)(2,1)}), bf16[32,1,5,1024]{3,2,1,0:T(8,128)(2,1)}, u32[]{:S(2)}, u32[]{:S(2)}) async-start(bf16[32,1,5,1024]{3,2,1,0:T(8,128)(2,1)} %copy.34), calls=%async_computation.4 | async-start | bytes 1048576 | tf_op jit(solution)/shard_map/all_to_all | solution.py:92
  163.5 67.7 %all-gather.5.cloned.1.call-start = ((), (), s32[]{:S(2)}) async-start(), calls=%async_computation.12 | async-start | bytes 3538944 | tf_op jit(solution)/shard_map/all_gather | solution.py:76
  181.6 3.3 copy-start.5
  206.6 83.3 %reduce-scatter.5.cloned.1.call-start = ((), (), s32[]{:S(2)}) async-start(), calls=%async_computation.13 | async-start | bytes 3538944 | tf_op jit(solution)/shard_map/reduce_scatter | solution.py:83
  284.5 41.8 %copy-start.2 = (bf16[1024,64]{0,1:T(8,128)(2,1)S(1)}, bf16[1024,64]{0,1:T(8,128)(2,1)}, u32[]{:S(2)}) copy-start(bf16[1024,64]{0,1:T(8,128)(2,1)} %param.21) | copy-start | bytes 393220
  284.5 31.7 %all-to-all-start.5 = ((bf16[8,128,1024]{2,1,0:T(8,128)(2,1)}), bf16[8,128,1024]{2,1,0:T(8,128)(2,1)}, u32[]{:S(2)}, u32[]{:S(2)}) async-start(bf16[8,128,1024]{2,1,0:T(8,128)(2,1)} %bitcast.96), calls=%async_computation.6 | async-start | bytes 4194304 | tf_op jit(solution)/shard_map/all_to_all | solution.py:29
  316.1 24.5 %all-to-all-start.7 = ((bf16[32,2,3,1024]{3,1,2,0:T(2,128)(2,1)}), bf16[32,2,3,1024]{3,1,2,0:T(2,128)(2,1)S(1)}, u32[]{:S(2)}, u32[]{:S(2)}) async-start(bf16[32,2,3,1024]{3,1,2,0:T(2,128)(2,1)} %copy.37), calls=%async_computation.9 | async-start | bytes 786432 | tf_op jit(solution)/shard_map/all_to_all | solution.py:92
Sparse Core Ops, SparseCore 0:
  42.7 24.9 all-gather.2
  75.0 49.9 reduce-scatter.2
  206.7 24.4 all-gather.4
  239.2 50.5 reduce-scatter.4
where the time goes:
time: 355 us; the launch traced here: 354 us
  blocking collectives  125 us (35%)
  waiting for transfers between devices  124 us (35%)
  starting transfers between devices  29.5 us (8%)
  matrix products  27.8 us (8%)
  other arithmetic  18.2 us (5%)
  local copies, waits for them, and re-layouts  15.4 us (4%)
  between operations  13.4 us (4%)
    all_to_all x2, blocking collectives, from_everyone(): return lax.all_to_all(copies, axis, split_axis=0, concat_axis=0, tiled=True)  78 us
    all_gather x2, waiting for transfers between devices, moe_layer(): lax.all_gather(arrived, 'dp', axis=0, tiled=True)  49.5 us
    all_to_all x2, waiting for transfers between devices, summed_on_arrival(): lax.all_to_all(in_blocks(value, dim, devices), axis, 0, 0, tiled=True)  48.7 us
    all_to_all x2, blocking collectives, moe_layer(): lax.all_to_all(buffer, 'expert', split_axis=0, concat_axis=0, tiled=True)  47.2 us
    all_to_all x2, waiting for transfers between devices, moe_layer(): lax.all_to_all(partial_value.astype(jnp.bfloat16), 'expert', split_axis=0...  25.4 us
    all_to_all x2, starting transfers between devices, moe_layer(): lax.all_to_all(partial_value.astype(jnp.bfloat16), 'expert', split_axis=0...  20.2 us
    dot_general x2, matrix products, moe_layer(): jnp.einsum('secf,efd->secd', rows, e_out, preferred_element_type=jnp.floa...  15 us
    dot_general x2, matrix products, moe_layer(): jnp.dot(rows, d_out, preferred_element_type=jnp.float32)  12.4 us
  transfers between devices with their start and end apart: 8, of which 7 were waited for; matrix products, arithmetic and copies ran while one was open for 7% of the time, Pallas kernels for 0%

commit v1 on v0

--- a/solution.py
+++ b/solution.py
@@ -70,12 +70,38 @@
     buffer = jnp.zeros((total, width), jnp.bfloat16).at[slot_row].set(normed, mode="drop")
     buffer = buffer.reshape(owners, per_dev, cap, width)
     arrived = lax.all_to_all(buffer, "expert", split_axis=0, concat_axis=0, tiled=True)
+
+    def test_map(my_tile, at_axis, local, ndim_at):
+        y1, outer, tile_out = (lax.axis_size("dp"), lax.axis_index("dp"), my_tile.shape[at_axis])
+        lower, clean = ([], [])
+        fresh = last = my_tile
+        for hop_no in range(y1 // 2 + 1):
+            lower.append(local(fresh, (outer - hop_no) % y1 * tile_out))
+            if 0 < hop_no < y1 - y1 // 2:
+                clean.append(local(last, (outer + hop_no) % y1 * tile_out))
+            fresh = lax.ppermute(
+                fresh, "dp", list(map(lambda tick: (tick, (tick + 1) % y1), range(y1)))
+            )
+            last = lax.ppermute(
+                last,
+                axis_name="dp",
+                perm=list(map(lambda tick: (tick, (tick - 1) % y1), range(y1))),
+            )
+        front = jnp.roll(
+            jnp.concatenate([*lower[::-1], *clean], axis=ndim_at),
+            (outer - y1 // 2) * lower[0].shape[ndim_at],
+            ndim_at,
+        )
+        return front
+
     expert_act = jax.nn.gelu(
-        jnp.einsum(
-            "secd,edf->secf",
-            lax.all_gather(arrived, "dp", axis=0, tiled=True),
-            e_in,
-            preferred_element_type=jnp.float32,
+        test_map(
+            arrived,
+            0,
+            lambda shard, start: jnp.einsum(
+                "secd,edf->secf", shard, e_in, preferred_element_type=jnp.float32
+            ),
+            0,
         ),
         approximate=True,
     ).astype(jnp.bfloat16)

time: 355 us -> 368 us (1.037)
  starting transfers between devices: 29.5 us -> 36.4 us
  blocking collectives: 125 us -> 129 us
    all_gather x2 -> x0, waiting for transfers between devices: 49.5 us -> none  [moe_layer(): lax.all_gather(arrived, 'dp', axis=0, tiled=True)]
    ppermute x0 -> x14, waiting for transfers between devices: none -> 46.9 us  [the longest x8 46.7 us: test_map(): lax.ppermute(fresh, 'dp', list(map(lambda tick: (tick, (tick + 1) % y1),...]
    ppermute x0 -> x14, starting transfers between devices: none -> 18 us  [the longest x6 18 us: test_map(): lax.ppermute(last, axis_name='dp', perm=list(map(lambda tick: (tick, (tic...]
    all_to_all x2, starting transfers between devices: 20.2 us -> 9.35 us  [moe_layer(): lax.all_to_all(partial_value.astype(jnp.bfloat16), 'expert', split_axis=0...]
    dot_general x0 -> x16, matrix products: none -> 10.4 us  [moe_layer(): jnp.einsum('secd,edf->secf', shard, e_in, preferred_element_type=jnp.floa...]
    dot_general x2, matrix products: 15 us -> 6.95 us  [moe_layer(): jnp.einsum('secf,efd->secd', rows, e_out, preferred_element_type=jnp.floa...]
    all_to_all x2, blocking collectives: 78 us -> 82 us  [from_everyone(): return lax.all_to_all(copies, axis, split_axis=0, concat_axis=0, tiled=True)]
  transfers between devices with their start and end apart: 8 -> 20, of which waited for: 7 -> 13; matrix products, arithmetic and copies ran while one was open for 7% -> 9% of each run, Pallas kernels for 0% -> 0%
where the time goes in v1:
time: 368 us; the launch traced here: 367 us
  blocking collectives  129 us (35%)
  waiting for transfers between devices  123 us (33%)
  starting transfers between devices  36.4 us (10%)
  matrix products  30.1 us (8%)
  other arithmetic  18.3 us (5%)
  local copies, waits for them, and re-layouts  16.2 us (4%)
  between operations  14 us (4%)
    all_to_all x2, blocking collectives, from_everyone(): return lax.all_to_all(copies, axis, split_axis=0, concat_axis=0, tiled=True)  82 us
    all_to_all x2, waiting for transfers between devices, summed_on_arrival(): lax.all_to_all(in_blocks(value, dim, devices), axis, 0, 0, tiled=True)  49.5 us
    all_to_all x2, blocking collectives, moe_layer(): lax.all_to_all(buffer, 'expert', split_axis=0, concat_axis=0, tiled=True)  47.3 us
    ppermute x8, waiting for transfers between devices, test_map(): lax.ppermute(fresh, 'dp', list(map(lambda tick: (tick, (tick + 1) % y1),...  46.7 us
    all_to_all x2, waiting for transfers between devices, moe_layer(): lax.all_to_all(partial_value.astype(jnp.bfloat16), 'expert', split_axis=0...  26.1 us
    ppermute x6, starting transfers between devices, test_map(): lax.ppermute(last, axis_name='dp', perm=list(map(lambda tick: (tick, (tic...  18 us
    dot_general x2, matrix products, moe_layer(): jnp.dot(rows, d_out, preferred_element_type=jnp.float32)  12.4 us
    dot_general x16, matrix products, moe_layer(): jnp.einsum('secd,edf->secf', shard, e_in, preferred_element_type=jnp.floa...  10.4 us
  transfers between devices with their start and end apart: 20, of which 13 were waited for; matrix products, arithmetic and copies ran while one was open for 9% of the time, Pallas kernels for 0%

profile of v1, /device:TPU:32, one launch (start us, length us, event | category | flops | bytes accessed | tf_op | source)
XLA Modules:
  0.0 366.9 jit_solution(5394407073262144370)
XLA Ops:
  6.5 0.9 fusion.131
  7.6 0.8 select_reduce_fusion.1
  8.4 0.7 and_bitcast_fusion.1
  9.1 1.1 convert_reduce_fusion.3
  10.2 1.2 fusion.111
  11.4 1.8 scatter_custom_fusion
  13.1 0.9 reshape.356
  14.1 28.6 %all_to_all.40 = bf16[32,1,5,1024]{3,2,1,0:T(8,128)(2,1)S(1)} all-to-all(bf16[32,1,5,1024]{3,2,1,0:T(8,128)(2,1)} %bitcast.255), channel_id=1, replica_groups=mesh['dp'=8,'expert'=32] {'expert'}, dimensions={0} | all-to-all | bytes 655360 | tf_op jit(solution)/shard_map/all_to_all | solution.py:72
  42.9 7.7 %collective-permute-done = bf16[32,1,5,1024]{3,0,2,1:T(8,128)(2,1)S(1)} collective-permute-done((bf16[32,1,5,1024]{3,0,2,1:T(8,128)(2,1)S(1)}, bf16[32,1,5,1024]{3,0,2,1:T(8,128)(2,1)S(1)}, u32[]{:S(2)}, u32[]{:S(2)}) %collective-permute-start) | collective-permute-done | bytes 327712 | tf_op jit(solution)/shard_map/ppermute | solution.py:82
  50.6 3.0 collective-permute-start.4
  53.5 4.8 %collective-permute-done.1 = bf16[32,1,5,1024]{3,0,2,1:T(8,128)(2,1)S(1)} collective-permute-done((bf16[32,1,5,1024]{3,0,2,1:T(8,128)(2,1)S(1)}, bf16[32,1,5,1024]{3,0,2,1:T(8,128)(2,1)S(1)}, u32[]{:S(2)}, u32[]{:S(2)}) %collective-permute-start.1) | collective-permute-done | bytes 327712 | tf_op jit(solution)/shard_map/ppermute | solution.py:82
  58.3 3.0 collective-permute-start.5
  61.3 4.7 %collective-permute-done.2 = bf16[32,1,5,1024]{3,0,2,1:T(8,128)(2,1)} collective-permute-done((bf16[32,1,5,1024]{3,0,2,1:T(8,128)(2,1)S(1)}, bf16[32,1,5,1024]{3,0,2,1:T(8,128)(2,1)}, u32[]{:S(2)}, u32[]{:S(2)}) %collective-permute-start.2) | collective-permute-done | bytes 327712 | tf_op jit(solution)/shard_map/ppermute | solution.py:82
  66.3 3.1 collective-permute-start.6
  69.4 4.8 %collective-permute-done.3 = bf16[32,1,5,1024]{3,0,2,1:T(8,128)(2,1)} collective-permute-done((bf16[32,1,5,1024]{3,0,2,1:T(8,128)(2,1)}, bf16[32,1,5,1024]{3,0,2,1:T(8,128)(2,1)}, u32[]{:S(2)}, u32[]{:S(2)}) %collective-permute-start.3) | collective-permute-done | bytes 327712 | tf_op jit(solution)/shard_map/ppermute | solution.py:82
  74.1 1.3 constant_dynamic-update-slice_fusion.15
  75.4 1.3 constant_dynamic-update-slice_fusion.14
  77.8 1.3 constant_dynamic-update-slice_fusion.10
  79.2 1.3 constant_dynamic-update-slice_fusion.9
  80.5 0.3 constant_dynamic-update-slice_fusion.8
  81.1 0.6 copy-done.14
  81.7 3.3 convert_bitcast_fusion.1
  85.5 40.4 %all_to_all.41 = bf16[8,128,1024]{2,1,0:T(8,128)(2,1)} all-to-all(bf16[8,128,1024]{2,1,0:T(8,128)(2,1)S(1)} %broadcast_in_dim.49), channel_id=1, replica_groups=mesh['dp'=8,'expert'=32] {'dp'}, dimensions={0} | all-to-all | bytes 4194304 | tf_op jit(solution)/shard_map/all_to_all | solution.py:15
  125.9 6.2 %convolution_convert_fusion.1 = bf16[1024,1024]{1,0:T(8,128)(2,1)} fusion(bf16[512,1024]{1,0:T(8,128)(2,1)} %param.23, bf16[1024,1024]{1,0:T(8,128)(2,1)} %bitcast.253, bf16[1024,512]{1,0:T(8,128)(2,1)} %param.22), kind=kOutput, calls=%fused_computation.62 | convolution fusion | flops 2153250816 | bytes 6291456 | tf_op jit(solution)/shard_map/dot_general | solution.py:68
  132.1 4.5 %all-to-all-start.1 = ((bf16[8,128,1024]{2,1,0:T(8,128)(2,1)}), bf16[8,128,1024]{2,1,0:T(8,128)(2,1)}, u32[]{:S(2)}, u32[]{:S(2)}) async-start(bf16[8,128,1024]{2,1,0:T(8,128)(2,1)} %bitcast.251), calls=%async_computation.1 | async-start | bytes 4194304 | tf_op jit(solution)/shard_map/all_to_all | solution.py:29
  137.4 2.0 copy.44
  139.3 24.5 %all-to-all-done.1 = bf16[8,128,1024]{2,1,0:T(8,128)(2,1)} async-done(((bf16[8,128,1024]{2,1,0:T(8,128)(2,1)}), bf16[8,128,1024]{2,1,0:T(8,128)(2,1)}, u32[]{:S(2)}, u32[]{:S(2)}) %all-to-all-start.1) | async-done | bytes 2097184 | tf_op jit(solution)/shard_map/all_to_all | solution.py:29
  163.8 5.2 %all-to-all-start.3 = ((bf16[32,1,5,1024]{3,2,1,0:T(8,128)(2,1)}), bf16[32,1,5,1024]{3,2,1,0:T(8,128)(2,1)}, u32[]{:S(2)}, u32[]{:S(2)}) async-start(bf16[32,1,5,1024]{3,2,1,0:T(8,128)(2,1)} %copy.44), calls=%async_computation.4 | async-start | bytes 1048576 | tf_op jit(solution)/shard_map/all_to_all | solution.py:118
  169.1 2.8 convert_reduce_fusion.1
  171.9 14.4 %all-to-all-done.3 = bf16[32,1,5,1024]{3,2,1,0:T(8,128)(2,1)} async-done(((bf16[32,1,5,1024]{3,2,1,0:T(8,128)(2,1)}), bf16[32,1,5,1024]{3,2,1,0:T(8,128)(2,1)}, u32[]{:S(2)}, u32[]{:S(2)}) %all-to-all-start.3) | async-done | bytes 327712 | tf_op jit(solution)/shard_map/all_to_all | solution.py:118
  186.3 1.2 reshape.376
  187.5 1.6 gather_fusion
  189.1 1.4 convert_reduce_fusion.2
  190.8 1.6 scatter_custom_fusion.1
  192.9 18.7 %all_to_all.42 = bf16[32,2,3,1024]{3,1,2,0:T(2,128)(2,1)S(1)} all-to-all(bf16[32,2,3,1024]{3,1,2,0:T(2,128)(2,1)S(1)} %copy.45), channel_id=1, replica_groups=mesh['dp'=8,'expert'=32] {'expert'}, dimensions={0} | all-to-all | bytes 786432 | tf_op jit(solution)/shard_map/all_to_all | solution.py:72
  211.8 8.4 %collective-permute-done.7 = bf16[32,2,3,1024]{3,0,2,1:T(8,128)(2,1)S(1)} collective-permute-done((bf16[32,2,3,1024]{3,0,2,1:T(8,128)(2,1)S(1)}, bf16[32,2,3,1024]{3,0,2,1:T(8,128)(2,1)S(1)}, u32[]{:S(2)}, u32[]{:S(2)}) %collective-permute-start.7) | collective-permute-done | bytes 393248 | tf_op jit(solution)/shard_map/ppermute | solution.py:82
  220.2 3.0 collective-permute-start.11
  223.1 5.5 %collective-permute-done.8 = bf16[32,2,3,1024]{3,0,2,1:T(8,128)(2,1)S(1)} collective-permute-done((bf16[32,2,3,1024]{3,0,2,1:T(8,128)(2,1)S(1)}, bf16[32,2,3,1024]{3,0,2,1:T(8,128)(2,1)S(1)}, u32[]{:S(2)}, u32[]{:S(2)}) %collective-permute-start.8) | collective-permute-done | bytes 393248 | tf_op jit(solution)/shard_map/ppermute | solution.py:82
  228.6 3.0 collective-permute-start.12
  231.5 5.5 %collective-permute-done.9 = bf16[32,2,3,1024]{3,0,2,1:T(8,128)(2,1)S(1)} collective-permute-done((bf16[32,2,3,1024]{3,0,2,1:T(8,128)(2,1)S(1)}, bf16[32,2,3,1024]{3,0,2,1:T(8,128)(2,1)S(1)}, u32[]{:S(2)}, u32[]{:S(2)}) %collective-permute-start.9) | collective-permute-done | bytes 393248 | tf_op jit(solution)/shard_map/ppermute | solution.py:82
  237.0 3.0 collective-permute-start.13
  239.9 5.5 %collective-permute-done.10 = bf16[32,2,3,1024]{3,0,2,1:T(8,128)(2,1)S(1)} collective-permute-done((bf16[32,2,3,1024]{3,0,2,1:T(8,128)(2,1)S(1)}, bf16[32,2,3,1024]{3,0,2,1:T(8,128)(2,1)S(1)}, u32[]{:S(2)}, u32[]{:S(2)}) %collective-permute-start.10) | collective-permute-done | bytes 393248 | tf_op jit(solution)/shard_map/ppermute | solution.py:82
  245.4 0.5 constant_dynamic-update-slice_fusion.31
  245.9 0.5 constant_dynamic-update-slice_fusion.30
  246.3 0.5 constant_dynamic-update-slice_fusion.29
  246.8 0.5 constant_dynamic-update-slice_fusion.28
  247.3 0.5 constant_dynamic-update-slice_fusion.27
  247.7 0.5 constant_dynamic-update-slice_fusion.26
  248.2 0.5 constant_dynamic-update-slice_fusion.25
  248.7 0.5 constant_dynamic-update-slice_fusion.24
  249.5 1.3 copy-done.13
  250.8 3.7 %convert_bitcast_fusion = bf16[256,2,3,1024]{3,0,2,1:T(8,128)(2,1)} fusion(bf16[2,512,1024]{2,1,0:T(8,128)(2,1)S(1)} %copy-done.13, f32[512,2,3,512]{3,0,2,1:T(8,128)S(1)} %constant_dynamic-update-slice_fusion.16, s32[]{:T(128)S(6)} %select_n.56), kind=kOutput, calls=%fused_computation.16 | convolution fusion | flops 1619263488 | bytes 8388612 | tf_op jit(solution)/shard_map/secf,efd->secd/dot_general | solution.py:110
  254.9 41.5 %all_to_all.43 = bf16[8,128,1024]{2,1,0:T(8,128)(2,1)} all-to-all(bf16[8,128,1024]{2,1,0:T(8,128)(2,1)S(1)} %broadcast_in_dim.54), channel_id=1, replica_groups=mesh['dp'=8,'expert'=32] {'dp'}, dimensions={0} | all-to-all | bytes 4194304 | tf_op jit(solution)/shard_map/all_to_all | solution.py:15
  296.5 6.2 %convolution_convert_fusion = bf16[1024,1024]{1,0:T(8,128)(2,1)} fusion(bf16[512,1024]{1,0:T(8,128)(2,1)} %param.25, bf16[1024,1024]{1,0:T(8,128)(2,1)} %bitcast.254, bf16[1024,512]{1,0:T(8,128)(2,1)} %param.24), kind=kOutput, calls=%fused_computation.61 | convolution fusion | flops 2153250816 | bytes 6291456 | tf_op jit(solution)/shard_map/dot_general | solution.py:68
  302.7 4.5 %all-to-all-start.5 = ((bf16[8,128,1024]{2,1,0:T(8,128)(2,1)}), bf16[8,128,1024]{2,1,0:T(8,128)(2,1)}, u32[]{:S(2)}, u32[]{:S(2)}) async-start(bf16[8,128,1024]{2,1,0:T(8,128)(2,1)} %bitcast.252), calls=%async_computation.6 | async-start | bytes 4194304 | tf_op jit(solution)/shard_map/all_to_all | solution.py:29
  307.2 2.2 copy.49
  309.3 25.0 %all-to-all-done.5 = bf16[8,128,1024]{2,1,0:T(8,128)(2,1)} async-done(((bf16[8,128,1024]{2,1,0:T(8,128)(2,1)}), bf16[8,128,1024]{2,1,0:T(8,128)(2,1)}, u32[]{:S(2)}, u32[]{:S(2)}) %all-to-all-start.5) | async-done | bytes 2097184 | tf_op jit(solution)/shard_map/all_to_all | solution.py:29
  334.3 4.2 %all-to-all-start.7 = ((bf16[32,2,3,1024]{3,1,2,0:T(2,128)(2,1)}), bf16[32,2,3,1024]{3,1,2,0:T(2,128)(2,1)S(1)}, u32[]{:S(2)}, u32[]{:S(2)}) async-start(bf16[32,2,3,1024]{3,1,2,0:T(2,128)(2,1)} %copy.49), calls=%async_computation.9 | async-start | bytes 786432 | tf_op jit(solution)/shard_map/all_to_all | solution.py:118
  338.8 2.8 convert_reduce_fusion
  341.6 11.7 %all-to-all-done.7 = bf16[32,2,3,1024]{3,1,2,0:T(2,128)(2,1)S(1)} async-done(((bf16[32,2,3,1024]{3,1,2,0:T(2,128)(2,1)}), bf16[32,2,3,1024]{3,1,2,0:T(2,128)(2,1)S(1)}, u32[]{:S(2)}, u32[]{:S(2)}) %all-to-all-start.7) | async-done | bytes 393248 | tf_op jit(solution)/shard_map/all_to_all | solution.py:118
  353.4 1.5 copy.51
  354.9 1.6 reshape.378
  356.5 1.6 gather_fusion.1
  358.1 2.0 fusion.117
  (92 shorter events, 4.9 us)
Async XLA Ops:
  6.5 238.9 %copy-start = (bf16[2,1024,512]{2,1,0:T(8,128)(2,1)S(1)}, bf16[2,1024,512]{2,1,0:T(8,128)(2,1)}, u32[]{:S(2)}) copy-start(bf16[2,1024,512]{2,1,0:T(8,128)(2,1)} %param.28) | copy-start | bytes 6291460
  6.5 67.6 %copy-start.1 = (bf16[1,1024,512]{2,1,0:T(8,128)(2,1)S(1)}, bf16[1,1024,512]{2,1,0:T(8,128)(2,1)}, u32[]{:S(2)}) copy-start(bf16[1,1024,512]{2,1,0:T(8,128)(2,1)} %param.26) | copy-start | bytes 3145732
  6.5 130.8 %reduce-scatter.3.cloned.1.call-start = ((), (), s32[]{:S(2)}) async-start(), calls=%async_computation.10 | async-start | bytes 2949120 | tf_op jit(solution)/shard_map/reduce_scatter | solution.py:109
  42.8 7.7 %collective-permute-start = (bf16[32,1,5,1024]{3,0,2,1:T(8,128)(2,1)S(1)}, bf16[32,1,5,1024]{3,0,2,1:T(8,128)(2,1)S(1)}, u32[]{:S(2)}, u32[]{:S(2)}) collective-permute-start(bf16[32,1,5,1024]{3,0,2,1:T(8,128)(2,1)S(1)} %copy.41), channel_id=1, source_target_pairs={{0,32},{32,64},{64,96},{96,128},{128,160},{160,192},{192,224},{224... | collective-permute-start | bytes 983048 | tf_op jit(solution)/shard_map/ppermute | solution.py:82
  50.6 7.7 %copy-start.3 = (bf16[32,1,5,1024]{3,0,2,1:T(8,128)(2,1)}, bf16[32,1,5,1024]{3,0,2,1:T(8,128)(2,1)S(1)}, u32[]{:S(2)}) copy-start(bf16[32,1,5,1024]{3,0,2,1:T(8,128)(2,1)S(1)} %collective-permute-done) | copy-start | bytes 983044
  50.6 7.7 %collective-permute-start.1 = (bf16[32,1,5,1024]{3,0,2,1:T(8,128)(2,1)S(1)}, bf16[32,1,5,1024]{3,0,2,1:T(8,128)(2,1)S(1)}, u32[]{:S(2)}, u32[]{:S(2)}) collective-permute-start(bf16[32,1,5,1024]{3,0,2,1:T(8,128)(2,1)S(1)} %collective-permute-done), channel_id=1, source_target_pairs={{0,32},{32,64},{64,96},{96,128},{128,160},{160,192},{192,224},{224... | collective-permute-start | bytes 983048 | tf_op jit(solution)/shard_map/ppermute | solution.py:82
  50.6 7.7 %collective-permute-start.4 = (bf16[32,1,5,1024]{3,0,2,1:T(8,128)(2,1)S(1)}, bf16[32,1,5,1024]{3,0,2,1:T(8,128)(2,1)}, u32[]{:S(2)}, u32[]{:S(2)}) collective-permute-start(bf16[32,1,5,1024]{3,0,2,1:T(8,128)(2,1)S(1)} %copy.41), channel_id=1, source_target_pairs={{0,224},{32,0},{64,32},{96,64},{128,96},{160,128},{192,160},{224,1... | collective-permute-start | bytes 983048 | tf_op jit(solution)/shard_map/ppermute | solution.py:85
  58.3 3.1 copy-start.5
  58.3 7.8 %collective-permute-start.2 = (bf16[32,1,5,1024]{3,0,2,1:T(8,128)(2,1)S(1)}, bf16[32,1,5,1024]{3,0,2,1:T(8,128)(2,1)}, u32[]{:S(2)}, u32[]{:S(2)}) collective-permute-start(bf16[32,1,5,1024]{3,0,2,1:T(8,128)(2,1)S(1)} %collective-permute-done.1), channel_id=1, source_target_pairs={{0,32},{32,64},{64,96},{96,128},{128,160},{160,192},{192,224},{224... | collective-permute-start | bytes 983048 | tf_op jit(solution)/shard_map/ppermute | solution.py:82
  58.3 8.0 %collective-permute-start.5 = (bf16[32,1,5,1024]{3,0,2,1:T(8,128)(2,1)}, bf16[32,1,5,1024]{3,0,2,1:T(8,128)(2,1)}, u32[]{:S(2)}, u32[]{:S(2)}) collective-permute-start(bf16[32,1,5,1024]{3,0,2,1:T(8,128)(2,1)} %collective-permute-done.4), channel_id=1, source_target_pairs={{0,224},{32,0},{64,32},{96,64},{128,96},{160,128},{192,160},{224,1... | collective-permute-start | bytes 983048 | tf_op jit(solution)/shard_map/ppermute | solution.py:85
  66.1 8.0 %collective-permute-start.3 = (bf16[32,1,5,1024]{3,0,2,1:T(8,128)(2,1)}, bf16[32,1,5,1024]{3,0,2,1:T(8,128)(2,1)}, u32[]{:S(2)}, u32[]{:S(2)}) collective-permute-start(bf16[32,1,5,1024]{3,0,2,1:T(8,128)(2,1)} %collective-permute-done.2), channel_id=1, source_target_pairs={{0,32},{32,64},{64,96},{96,128},{128,160},{160,192},{192,224},{224... | collective-permute-start | bytes 983048 | tf_op jit(solution)/shard_map/ppermute | solution.py:82
  66.1 10.7 %copy-start.6 = (bf16[32,1,5,1024]{3,0,2,1:T(8,128)(2,1)S(1)}, bf16[32,1,5,1024]{3,0,2,1:T(8,128)(2,1)}, u32[]{:S(2)}) copy-start(bf16[32,1,5,1024]{3,0,2,1:T(8,128)(2,1)} %copy-done.5) | copy-start | bytes 983044
  66.1 11.0 %copy-start.4 = (bf16[32,1,5,1024]{3,0,2,1:T(8,128)(2,1)S(1)}, bf16[32,1,5,1024]{3,0,2,1:T(8,128)(2,1)}, u32[]{:S(2)}) copy-start(bf16[32,1,5,1024]{3,0,2,1:T(8,128)(2,1)} %copy-done.3) | copy-start | bytes 983044
  66.3 14.2 %collective-permute-start.6 = (bf16[32,1,5,1024]{3,0,2,1:T(8,128)(2,1)}, bf16[32,1,5,1024]{3,0,2,1:T(8,128)(2,1)S(1)}, u32[]{:S(2)}, u32[]{:S(2)}) collective-permute-start(bf16[32,1,5,1024]{3,0,2,1:T(8,128)(2,1)} %collective-permute-done.5), channel_id=1, source_target_pairs={{0,224},{32,0},{64,32},{96,64},{128,96},{160,128},{192,160},{224,1... | collective-permute-start | bytes 983048 | tf_op jit(solution)/shard_map/ppermute | solution.py:85
  80.5 1.2 copy-start.14
  81.7 3.3 copy-start.2
  81.7 3.3 copy-start.9
  132.1 4.5 %copy-start.12 = (s32[128,1]{0,1:T(1,128)S(1)}, s32[128,1]{0,1:T(1,128)}, u32[]{:S(2)}) copy-start(s32[128,1]{0,1:T(1,128)} %param.17) | copy-start | bytes 1540
  132.1 5.0 %copy-start.8 = (bf16[1024,32]{0,1:T(8,128)(2,1)S(1)}, bf16[1024,32]{0,1:T(8,128)(2,1)}, u32[]{:S(2)}) copy-start(bf16[1024,32]{0,1:T(8,128)(2,1)} %param.20) | copy-start | bytes 196612
  132.1 5.0 %copy-start.11 = (s32[128,1]{0,1:T(1,128)S(1)}, s32[128,1]{0,1:T(1,128)}, u32[]{:S(2)}) copy-start(s32[128,1]{0,1:T(1,128)} %param.16) | copy-start | bytes 1540
  132.1 31.7 %all-to-all-start.1 = ((bf16[8,128,1024]{2,1,0:T(8,128)(2,1)}), bf16[8,128,1024]{2,1,0:T(8,128)(2,1)}, u32[]{:S(2)}, u32[]{:S(2)}) async-start(bf16[8,128,1024]{2,1,0:T(8,128)(2,1)} %bitcast.251), calls=%async_computation.1 | async-start | bytes 4194304 | tf_op jit(solution)/shard_map/all_to_all | solution.py:29
  163.8 22.5 %all-to-all-start.3 = ((bf16[32,1,5,1024]{3,2,1,0:T(8,128)(2,1)}), bf16[32,1,5,1024]{3,2,1,0:T(8,128)(2,1)}, u32[]{:S(2)}, u32[]{:S(2)}) async-start(bf16[32,1,5,1024]{3,2,1,0:T(8,128)(2,1)} %copy.44), calls=%async_computation.4 | async-start | bytes 1048576 | tf_op jit(solution)/shard_map/all_to_all | solution.py:118
  169.0 138.2 %reduce-scatter.5.cloned.1.call-start = ((), (), s32[]{:S(2)}) async-start(), calls=%async_computation.11 | async-start | bytes 3538944 | tf_op jit(solution)/shard_map/reduce_scatter | solution.py:109
  187.5 3.3 copy-start.10
  211.7 8.4 %collective-permute-start.7 = (bf16[32,2,3,1024]{3,0,2,1:T(8,128)(2,1)S(1)}, bf16[32,2,3,1024]{3,0,2,1:T(8,128)(2,1)S(1)}, u32[]{:S(2)}, u32[]{:S(2)}) collective-permute-start(bf16[32,2,3,1024]{3,0,2,1:T(8,128)(2,1)S(1)} %copy.46), channel_id=1, source_target_pairs={{0,32},{32,64},{64,96},{96,128},{128,160},{160,192},{192,224},{224... | collective-permute-start | bytes 1179656 | tf_op jit(solution)/shard_map/ppermute | solution.py:82
  220.2 8.4 %collective-permute-start.8 = (bf16[32,2,3,1024]{3,0,2,1:T(8,128)(2,1)S(1)}, bf16[32,2,3,1024]{3,0,2,1:T(8,128)(2,1)S(1)}, u32[]{:S(2)}, u32[]{:S(2)}) collective-permute-start(bf16[32,2,3,1024]{3,0,2,1:T(8,128)(2,1)S(1)} %collective-permute-done.7), channel_id=1, source_target_pairs={{0,32},{32,64},{64,96},{96,128},{128,160},{160,192},{192,224},{224... | collective-permute-start | bytes 1179656 | tf_op jit(solution)/shard_map/ppermute | solution.py:82
  220.2 8.4 %collective-permute-start.11 = (bf16[32,2,3,1024]{3,0,2,1:T(8,128)(2,1)S(1)}, bf16[32,2,3,1024]{3,0,2,1:T(8,128)(2,1)S(1)}, u32[]{:S(2)}, u32[]{:S(2)}) collective-permute-start(bf16[32,2,3,1024]{3,0,2,1:T(8,128)(2,1)S(1)} %copy.46), channel_id=1, source_target_pairs={{0,224},{32,0},{64,32},{96,64},{128,96},{160,128},{192,160},{224,1... | collective-permute-start | bytes 1179656 | tf_op jit(solution)/shard_map/ppermute | solution.py:85
  228.6 8.4 %collective-permute-start.9 = (bf16[32,2,3,1024]{3,0,2,1:T(8,128)(2,1)S(1)}, bf16[32,2,3,1024]{3,0,2,1:T(8,128)(2,1)S(1)}, u32[]{:S(2)}, u32[]{:S(2)}) collective-permute-start(bf16[32,2,3,1024]{3,0,2,1:T(8,128)(2,1)S(1)} %collective-permute-done.8), channel_id=1, source_target_pairs={{0,32},{32,64},{64,96},{96,128},{128,160},{160,192},{192,224},{224... | collective-permute-start | bytes 1179656 | tf_op jit(solution)/shard_map/ppermute | solution.py:82
  228.6 8.4 %collective-permute-start.12 = (bf16[32,2,3,1024]{3,0,2,1:T(8,128)(2,1)S(1)}, bf16[32,2,3,1024]{3,0,2,1:T(8,128)(2,1)S(1)}, u32[]{:S(2)}, u32[]{:S(2)}) collective-permute-start(bf16[32,2,3,1024]{3,0,2,1:T(8,128)(2,1)S(1)} %collective-permute-done.11), channel_id=1, source_target_pairs={{0,224},{32,0},{64,32},{96,64},{128,96},{160,128},{192,160},{224,1... | collective-permute-start | bytes 1179656 | tf_op jit(solution)/shard_map/ppermute | solution.py:85
  237.0 8.4 %collective-permute-start.10 = (bf16[32,2,3,1024]{3,0,2,1:T(8,128)(2,1)S(1)}, bf16[32,2,3,1024]{3,0,2,1:T(8,128)(2,1)S(1)}, u32[]{:S(2)}, u32[]{:S(2)}) collective-permute-start(bf16[32,2,3,1024]{3,0,2,1:T(8,128)(2,1)S(1)} %collective-permute-done.9), channel_id=1, source_target_pairs={{0,32},{32,64},{64,96},{96,128},{128,160},{160,192},{192,224},{224... | collective-permute-start | bytes 1179656 | tf_op jit(solution)/shard_map/ppermute | solution.py:82
  237.0 11.7 %collective-permute-start.13 = (bf16[32,2,3,1024]{3,0,2,1:T(8,128)(2,1)S(1)}, bf16[32,2,3,1024]{3,0,2,1:T(8,128)(2,1)S(1)}, u32[]{:S(2)}, u32[]{:S(2)}) collective-permute-start(bf16[32,2,3,1024]{3,0,2,1:T(8,128)(2,1)S(1)} %collective-permute-done.12), channel_id=1, source_target_pairs={{0,224},{32,0},{64,32},{96,64},{128,96},{160,128},{192,160},{224,1... | collective-permute-start | bytes 1179656 | tf_op jit(solution)/shard_map/ppermute | solution.py:85
  249.2 1.6 copy-start.13
  302.6 35.9 %copy-start.7 = (bf16[1024,64]{0,1:T(8,128)(2,1)S(1)}, bf16[1024,64]{0,1:T(8,128)(2,1)}, u32[]{:S(2)}) copy-start(bf16[1024,64]{0,1:T(8,128)(2,1)} %param.21) | copy-start | bytes 393220
  302.7 31.7 %all-to-all-start.5 = ((bf16[8,128,1024]{2,1,0:T(8,128)(2,1)}), bf16[8,128,1024]{2,1,0:T(8,128)(2,1)}, u32[]{:S(2)}, u32[]{:S(2)}) async-start(bf16[8,128,1024]{2,1,0:T(8,128)(2,1)} %bitcast.252), calls=%async_computation.6 | async-start | bytes 4194304 | tf_op jit(solution)/shard_map/all_to_all | solution.py:29
  334.3 19.0 %all-to-all-start.7 = ((bf16[32,2,3,1024]{3,1,2,0:T(2,128)(2,1)}), bf16[32,2,3,1024]{3,1,2,0:T(2,128)(2,1)S(1)}, u32[]{:S(2)}, u32[]{:S(2)}) async-start(bf16[32,2,3,1024]{3,1,2,0:T(2,128)(2,1)} %copy.49), calls=%async_computation.9 | async-start | bytes 786432 | tf_op jit(solution)/shard_map/all_to_all | solution.py:118
Sparse Core Ops, SparseCore 0:
  85.1 47.5 reduce-scatter.2
  254.6 50.2 reduce-scatter.4
